TPU v7x, 32 devices: a whole 2x2x4 slice. The times are simulated.
32 devices in a mesh: seq: 4 (over z), tensor: 2 (over y), fsdp: 4 (over x, core).
Axes of the slice: x: 2, y: 2, z: 4, core: 2. Of those that a mesh axis runs over, the one named last changes fastest.
Arguments:
- hidden_in: bfloat16 [2048, 2048], P(('seq', 'fsdp'), 'tensor'), may hold values from -12 to 12
- out_cotangent: bfloat16 [2048, 2048], P(('seq', 'fsdp'), 'tensor'), may hold values from -6 to 6
- attn_norm_gain: float32 [2048], replicated, may hold values from 0.1 to 1.9
- attn_norm_bias: float32 [2048], replicated, may hold values from -3 to 3
- mlp_norm_gain: float32 [2048], replicated, may hold values from 0.1 to 1.9
- mlp_norm_bias: float32 [2048], replicated, may hold values from -3 to 3
- qkv_weight: bfloat16 [2048, 6144], P(('seq', 'fsdp'), 'tensor')
- qkv_bias: float32 [6144], P('tensor'), may hold values from -0.6 to 0.6
- proj_weight: bfloat16 [2048, 2048], P(('seq', 'fsdp'), 'tensor'), may hold values from -1.5 to 1.5
- proj_bias: float32 [2048], P('tensor'), may hold values from -3 to 3
- up_weight: bfloat16 [2048, 8192], P(('seq', 'fsdp'), 'tensor'), may hold values from -0.125 to 0.125
- up_bias: float32 [8192], P('tensor'), may hold values from -3 to 3
- down_weight: bfloat16 [2048, 8192], P(('seq', 'fsdp'), 'tensor'), may hold values from -0.0625 to 0.0625
- down_bias: float32 [2048], P('tensor'), may hold values from -3 to 3
Outputs:
- hidden_out: bfloat16 [2048, 2048], P(('seq', 'fsdp'), 'tensor')
- input_grad: bfloat16 [2048, 2048], P(('seq', 'fsdp'), 'tensor')
- attn_gain_grad: float32 [2048], replicated
- attn_bias_grad: float32 [2048], replicated
- mlp_gain_grad: float32 [2048], replicated
- mlp_bias_grad: float32 [2048], replicated
- qkv_weight_grad: float32 [2048, 6144], P(('seq', 'fsdp'), 'tensor')
- qkv_bias_grad: float32 [6144], P('tensor')
- proj_weight_grad: float32 [2048, 2048], P(('seq', 'fsdp'), 'tensor')
- proj_bias_grad: float32 [2048], P('tensor')
- up_weight_grad: float32 [2048, 8192], P(('seq', 'fsdp'), 'tensor')
- up_bias_grad: float32 [8192], P('tensor')
- down_weight_grad: float32 [2048, 8192], P(('seq', 'fsdp'), 'tensor')
- down_bias_grad: float32 [2048], P('tensor')
All inputs are finite; a program needn't handle non-finite values.
Results may differ from a plain program's by a relative error of at most 0.013.
Values may be sent and summed in bfloat16 or wider, within the bound.
A program may use at most 256 MiB of HBM per device.

v0:
```python
import math
import jax
import jax.numpy as jnp
from jax import lax
from jax.sharding import PartitionSpec as P

HEAD_DIM = 256
ROT = 64
norm_eps = 1e-05
rope_base = 10000.0


def gelu_value(pre_act):
    return 0.5 * pre_act * (1.0 + lax.erf(pre_act * 0.7071067811865476))


def gelu_slope(pre_act):
    return (
        0.5 * (1.0 + lax.erf(pre_act * 0.7071067811865476))
        + pre_act * jnp.exp(-0.5 * pre_act * pre_act) * 0.3989422804014327
    )


def layer_norm_parts(row_values):
    centered = row_values - jnp.mean(row_values, axis=-1, keepdims=True)
    inv_std = lax.rsqrt(jnp.mean(centered * centered, axis=-1, keepdims=True) + norm_eps)
    return (centered * inv_std, inv_std)


def rotary_tables(positions):
    half_rot = ROT // 2
    exponent = jnp.arange(half_rot, dtype=jnp.float32) * (2.0 / ROT)
    frequency = jnp.exp(-exponent * math.log(rope_base))
    angles = positions.astype(jnp.float32)[:, None] * frequency[None, :]
    return (jnp.cos(angles), jnp.sin(angles))


def rotate_heads(values, cosine_table, sine_table):
    half_rot = ROT // 2
    first_half = values[..., :half_rot]
    second_half = values[..., half_rot:ROT]
    cos_part = cosine_table[:, None, :]
    sin_part = sine_table[:, None, :]
    return jnp.concatenate(
        [
            first_half * cos_part - second_half * sin_part,
            second_half * cos_part + first_half * sin_part,
            values[..., ROT:],
        ],
        axis=-1,
    )


def contract_rows(left_side, right_side):
    return lax.dot_general(
        left_side, right_side, (((0,), (0,)), ((), ())), preferred_element_type=jnp.float32
    )


def contract_cols(left_side, right_side):
    return lax.dot_general(
        left_side, right_side, (((1,), (1,)), ((), ())), preferred_element_type=jnp.float32
    )


def per_device(
    hidden_in,
    out_cotangent,
    attn_norm_gain,
    attn_norm_bias,
    mlp_norm_gain,
    mlp_norm_bias,
    qkv_weight,
    qkv_bias,
    proj_weight,
    proj_bias,
    up_weight,
    up_bias,
    down_weight,
    down_bias,
):
    seq_count = lax.axis_size("seq")
    fsdp_count = lax.axis_size("fsdp")
    seq_rank = lax.axis_index("seq")
    fsdp_rank = lax.axis_index("fsdp")
    tensor_rank = lax.axis_index("tensor")
    tok_rows = hidden_in.shape[0]
    local_width = hidden_in.shape[1]
    score_scale = HEAD_DIM ** (-0.5)
    rows_whole, grad_whole = (
        lax.all_gather(hidden_in, "tensor", axis=1, tiled=True),
        lax.all_gather(out_cotangent, "tensor", axis=1, tiled=True),
    )
    float_rows = rows_whole.astype(jnp.float32)
    normal_rows, inv_std = layer_norm_parts(float_rows)
    attn_in = (normal_rows * attn_norm_gain + attn_norm_bias).astype(jnp.bfloat16)
    mlp_in = (normal_rows * mlp_norm_gain + mlp_norm_bias).astype(jnp.bfloat16)
    qkv_full, proj_full, up_full, down_full = (
        lax.all_gather(qkv_weight, ("seq", "fsdp"), axis=0, tiled=True),
        lax.all_gather(proj_weight, ("seq", "fsdp"), axis=0, tiled=True),
        lax.all_gather(up_weight, ("seq", "fsdp"), axis=0, tiled=True),
        lax.all_gather(down_weight, ("seq", "fsdp"), axis=0, tiled=True),
    )
    local_heads = local_width // HEAD_DIM
    head_share = local_heads // seq_count
    qkv_rows = jnp.dot(attn_in, qkv_full, preferred_element_type=jnp.float32) + qkv_bias
    qkv_rows = qkv_rows.reshape(tok_rows, local_heads, 3, HEAD_DIM)
    positions = (seq_rank * fsdp_count + fsdp_rank) * tok_rows + jnp.arange(
        tok_rows, dtype=jnp.int32
    )
    cosine_table, sine_table = rotary_tables(positions)
    packed = jnp.concatenate(
        [
            rotate_heads(qkv_rows[:, :, 0], cosine_table, sine_table),
            rotate_heads(qkv_rows[:, :, 1], cosine_table, sine_table),
            qkv_rows[:, :, 2],
        ],
        axis=-1,
    ).astype(jnp.bfloat16)
    by_head = lax.all_to_all(packed, "seq", split_axis=1, concat_axis=0, tiled=True)
    head_rows = by_head.shape[0]
    query_heads = by_head[:, :, :HEAD_DIM]
    pair_local = by_head[:, :, HEAD_DIM:]
    row_index = jnp.arange(head_rows, dtype=jnp.int32)
    query_pos = (row_index // tok_rows * fsdp_count + fsdp_rank) * tok_rows + row_index % tok_rows
    pair_all = lax.all_gather(pair_local, "fsdp", axis=0, tiled=True)
    key_rows = pair_all.shape[0]
    key_index = jnp.arange(key_rows, dtype=jnp.int32)
    within = key_index % head_rows
    key_pos = (
        within // tok_rows * fsdp_count + key_index // head_rows
    ) * tok_rows + within % tok_rows
    block_keys = math.gcd(key_rows, 1024)
    block_numbers = jnp.arange(key_rows // block_keys, dtype=jnp.int32)

    def block_scores(pair_source, block_number):
        start_row = block_number * block_keys
        pair_block = lax.dynamic_slice_in_dim(pair_source, start_row, block_keys, 0)
        pos_block = lax.dynamic_slice_in_dim(key_pos, start_row, block_keys, 0)
        scores = (
            jnp.einsum(
                "rhd,khd->rhk",
                query_heads,
                pair_block[:, :, :HEAD_DIM],
                preferred_element_type=jnp.float32,
            )
            * score_scale
        )
        allowed = pos_block[None, None, :] <= query_pos[:, None, None]
        return (pair_block, jnp.where(allowed, scores, -1e30), allowed)

    def forward_step(running, block_number):
        running_max, running_sum, accumulated = running
        pair_block, scores, allowed = block_scores(pair_all, block_number)
        new_max = jnp.maximum(running_max, jnp.max(scores, axis=-1))
        exp_terms = jnp.where(allowed, jnp.exp(scores - new_max[..., None]), 0.0)
        rescale = jnp.exp(running_max - new_max)
        running_sum = running_sum * rescale + jnp.sum(exp_terms, axis=-1)
        accumulated = accumulated * rescale[..., None] + jnp.einsum(
            "rhk,khd->rhd",
            exp_terms.astype(jnp.bfloat16),
            pair_block[:, :, HEAD_DIM:],
            preferred_element_type=jnp.float32,
        )
        return ((new_max, running_sum, accumulated), None)

    start_max = jnp.full((head_rows, head_share), -1e30, jnp.float32)
    start_sum = jnp.zeros((head_rows, head_share), jnp.float32)
    start_acc = jnp.zeros((head_rows, head_share, HEAD_DIM), jnp.float32)
    (row_max, row_sum, accumulated), ignored = lax.scan(
        forward_step, (start_max, start_sum, start_acc), block_numbers
    )
    attn_out = (accumulated / row_sum[..., None]).astype(jnp.bfloat16)
    log_total = row_max + jnp.log(row_sum)
    attn_tokens = lax.all_to_all(attn_out, "seq", split_axis=0, concat_axis=1, tiled=True).reshape(
        tok_rows, local_width
    )
    attn_branch = contract_cols(attn_tokens, proj_full)
    up_rows = jnp.dot(mlp_in, up_full, preferred_element_type=jnp.float32) + up_bias
    active = gelu_value(up_rows).astype(jnp.bfloat16)
    mlp_branch = contract_cols(active, down_full)
    branch_cols = lax.psum_scatter(
        attn_branch + mlp_branch, "tensor", scatter_dimension=1, tiled=True
    )
    hidden_out = (hidden_in.astype(jnp.float32) + branch_cols + proj_bias + down_bias).astype(
        jnp.bfloat16
    )
    qkv_back, proj_back, up_back, down_back = (
        lax.all_gather(qkv_weight, ("seq", "fsdp"), axis=0, tiled=True),
        lax.all_gather(proj_weight, ("seq", "fsdp"), axis=0, tiled=True),
        lax.all_gather(up_weight, ("seq", "fsdp"), axis=0, tiled=True),
        lax.all_gather(down_weight, ("seq", "fsdp"), axis=0, tiled=True),
    )
    pair_back = lax.all_gather(pair_local, "fsdp", axis=0, tiled=True)
    head_grad = jnp.dot(grad_whole, proj_back, preferred_element_type=jnp.float32).astype(
        jnp.bfloat16
    )
    grad_heads = lax.all_to_all(
        head_grad.reshape(tok_rows, local_heads, HEAD_DIM),
        "seq",
        split_axis=1,
        concat_axis=0,
        tiled=True,
    )
    proj_term = contract_rows(grad_whole, attn_tokens)
    pre_grad = jnp.dot(grad_whole, down_back, preferred_element_type=jnp.float32) * gelu_slope(
        up_rows
    )
    pre_rounded = pre_grad.astype(jnp.bfloat16)
    up_bias_term = jnp.sum(pre_grad, axis=0)
    up_term = contract_rows(mlp_in, pre_rounded)
    down_term = contract_rows(grad_whole, active)
    mlp_in_grad = contract_cols(pre_rounded, up_back)
    row_delta = jnp.sum(grad_heads.astype(jnp.float32) * attn_out.astype(jnp.float32), axis=-1)

    def backward_step(query_grad, block_number):
        pair_block, scores, allowed = block_scores(pair_back, block_number)
        prob_weights = jnp.where(allowed, jnp.exp(scores - log_total[..., None]), 0.0)
        prob_grad = jnp.einsum(
            "rhd,khd->rhk",
            grad_heads,
            pair_block[:, :, HEAD_DIM:],
            preferred_element_type=jnp.float32,
        )
        score_grad = (prob_weights * (prob_grad - row_delta[..., None])).astype(jnp.bfloat16)
        query_grad = query_grad + jnp.einsum(
            "rhk,khd->rhd",
            score_grad,
            pair_block[:, :, :HEAD_DIM],
            preferred_element_type=jnp.float32,
        )
        key_term = (
            jnp.einsum("rhk,rhd->khd", score_grad, query_heads, preferred_element_type=jnp.float32)
            * score_scale
        )
        value_term = jnp.einsum(
            "rhk,rhd->khd",
            prob_weights.astype(jnp.bfloat16),
            grad_heads,
            preferred_element_type=jnp.float32,
        )
        return (query_grad, jnp.concatenate([key_term, value_term], axis=-1))

    query_grad, pair_terms = lax.scan(backward_step, start_acc, block_numbers)
    pair_terms = pair_terms.reshape(key_rows, head_share, 2 * HEAD_DIM)
    pair_grad = lax.psum_scatter(pair_terms, "fsdp", scatter_dimension=0, tiled=True)
    head_cos, head_sin = rotary_tables(query_pos)
    grads_packed = jnp.concatenate(
        [
            rotate_heads(query_grad * score_scale, head_cos, -head_sin),
            rotate_heads(pair_grad[:, :, :HEAD_DIM], head_cos, -head_sin),
            pair_grad[:, :, HEAD_DIM:],
        ],
        axis=-1,
    ).astype(jnp.bfloat16)
    token_grads = lax.all_to_all(
        grads_packed, "seq", split_axis=0, concat_axis=1, tiled=True
    ).reshape(tok_rows, 3 * local_width)
    qkv_bias_term = jnp.sum(token_grads.astype(jnp.float32), axis=0)
    qkv_term = contract_rows(attn_in, token_grads)
    attn_in_grad = contract_cols(token_grads, qkv_back)
    attn_in_grad, mlp_in_grad = lax.psum((attn_in_grad, mlp_in_grad), "tensor")
    attn_gain_term = jnp.sum(attn_in_grad * normal_rows, axis=0)
    attn_bias_term = jnp.sum(attn_in_grad, axis=0)
    mlp_gain_term = jnp.sum(mlp_in_grad * normal_rows, axis=0)
    mlp_bias_term = jnp.sum(mlp_in_grad, axis=0)
    spread_grad = attn_in_grad * attn_norm_gain + mlp_in_grad * mlp_norm_gain
    mean_grad = jnp.mean(spread_grad, axis=-1, keepdims=True)
    mean_proj = jnp.mean(spread_grad * normal_rows, axis=-1, keepdims=True)
    column_start = tensor_rank * local_width
    spread_cols = lax.dynamic_slice_in_dim(spread_grad, column_start, local_width, 1)
    normal_cols = lax.dynamic_slice_in_dim(normal_rows, column_start, local_width, 1)
    grad_local = out_cotangent.astype(jnp.float32)
    input_grad = (
        grad_local + inv_std * (spread_cols - mean_grad - normal_cols * mean_proj)
    ).astype(jnp.bfloat16)
    out_bias_term = jnp.sum(grad_local, axis=0)
    qkv_weight_grad, proj_weight_grad, up_weight_grad, down_weight_grad = (
        lax.psum_scatter(qkv_term, ("seq", "fsdp"), scatter_dimension=0, tiled=True),
        lax.psum_scatter(proj_term, ("seq", "fsdp"), scatter_dimension=0, tiled=True),
        lax.psum_scatter(up_term, ("seq", "fsdp"), scatter_dimension=0, tiled=True),
        lax.psum_scatter(down_term, ("seq", "fsdp"), scatter_dimension=0, tiled=True),
    )
    (
        qkv_bias_grad,
        out_bias_grad,
        up_bias_grad,
        attn_gain_grad,
        attn_bias_grad,
        mlp_gain_grad,
        mlp_bias_grad,
    ) = lax.psum(
        (
            qkv_bias_term,
            out_bias_term,
            up_bias_term,
            attn_gain_term,
            attn_bias_term,
            mlp_gain_term,
            mlp_bias_term,
        ),
        ("seq", "fsdp"),
    )
    return (
        hidden_out,
        input_grad,
        attn_gain_grad,
        attn_bias_grad,
        mlp_gain_grad,
        mlp_bias_grad,
        qkv_weight_grad,
        qkv_bias_grad,
        proj_weight_grad,
        out_bias_grad,
        up_weight_grad,
        up_bias_grad,
        down_weight_grad,
        out_bias_grad,
    )


def solution(mesh):
    placed = (
        P(("seq", "fsdp"), "tensor"),
        P(("seq", "fsdp"), "tensor"),
        P(),
        P(),
        P(),
        P(),
        P(("seq", "fsdp"), "tensor"),
        P("tensor"),
        P(("seq", "fsdp"), "tensor"),
        P("tensor"),
        P(("seq", "fsdp"), "tensor"),
        P("tensor"),
        P(("seq", "fsdp"), "tensor"),
        P("tensor"),
    )
    return jax.shard_map(
        per_device,
        mesh=mesh,
        in_specs=placed,
        out_specs=(
            P(("seq", "fsdp"), "tensor"),
            P(("seq", "fsdp"), "tensor"),
            P(),
            P(),
            P(),
            P(),
            P(("seq", "fsdp"), "tensor"),
            P("tensor"),
            P(("seq", "fsdp"), "tensor"),
            P("tensor"),
            P(("seq", "fsdp"), "tensor"),
            P("tensor"),
            P(("seq", "fsdp"), "tensor"),
            P("tensor"),
        ),
        check_vma=False,
    )
```

profile of v0, /device:TPU:0, one launch (start us, length us, event | category | flops | bytes accessed | tf_op | source)
XLA Modules:
  0.0 1770.2 jit_solution(5235780684351520265)
XLA Ops:
  8.8 10.2 all_gather.26
  19.6 93.9 %all-gather.6.cloned.1.call-done = bf16[2048,3072]{1,0:T(8,128)(2,1)} async-done(((bf16[128,3072]{1,0:T(8,128)(2,1)}), bf16[2048,3072]{1,0:T(8,128)(2,1)}) %all-gather.6.cloned.1.call-update) | async-done | bytes 12582928 | tf_op jit(solution)/shard_map/all_gather | solution.py:99
  113.5 6.5 convolution_add_fusion.1
  120.1 1.6 copy.90
  125.8 33.6 %all_to_all.66 = bf16[128,4,768]{2,0,1:T(8,128)(2,1)S(1)} all-to-all(bf16[128,4,768]{2,0,1:T(8,128)(2,1)S(1)} %concatenate.20), channel_id=1, replica_groups=mesh['seq'=4,'tensor'=2,'fsdp'=4] {'seq'}, dimensions={1} | all-to-all | bytes 1572864 | tf_op jit(solution)/shard_map/all_to_all | solution.py:120
  160.9 8.1 all_gather.32
  170.4 2.9 convolution_convert_fusion
  174.0 3.4 all-to-all-start.2
  177.5 16.9 all-gather.8.cloned.1.call-done
  194.4 11.1 while.28
  195.7 1.5 fusion.175
  197.9 2.0 fusion.179
  201.2 1.5 fusion.175
  203.4 2.1 fusion.179
  206.6 28.2 %while.29 = (s32[]{:T(128)}, f32[512,1,256]{0,2,1:T(8,128)}, f32[2,1024,1,512]{3,1,0,2:T(8,128)}, s32[2]{0:T(128)S(1)}, bf16[2048,1,512]{2,0,1:T(8,128)(2,1)}, /...) while((s32[]{:T(128)}, f32[512,1,256]{0,2,1:T(8,128)}, ...), condition=%wide.region_9.10_spmd.clone, body=%wide.region_8.9_spmd.clone.sunk | while | flops 1347952640 | bytes 34100076 | solution.py:244
  207.9 1.8 compare_select_fusion.5
  209.7 1.5 fusion.188
  211.3 1.4 fusion.190
  213.3 1.8 copy.132
  215.2 3.1 constant_dynamic-update-slice_fusion.2
  218.3 1.6 fusion.189
  222.0 1.8 compare_select_fusion.5
  223.8 1.5 fusion.188
  225.3 1.4 fusion.190
  227.4 1.8 copy.132
  229.2 3.2 constant_dynamic-update-slice_fusion.2
  232.4 1.6 fusion.189
  234.8 5.5 copy.104
  240.3 10.9 all-gather.14.cloned.1.call-start
  252.0 70.9 %all-gather.12.cloned.1.call-done = bf16[2048,4096]{1,0:T(8,128)(2,1)} async-done(((bf16[128,4096]{1,0:T(8,128)(2,1)}), bf16[2048,4096]{1,0:T(8,128)(2,1)}) %all-gather.12.cloned.1.call-update) | async-done | bytes 16777232 | tf_op jit(solution)/shard_map/all_gather | solution.py:101
  322.9 8.2 convolution_add_fusion
  331.1 36.7 %reduce-scatter.9.cloned.1.call-done = f32[512,1,512]{0,2,1:T(8,128)} async-done(((f32[2048,1,512]{0,2,1:T(8,128)}), f32[512,1,512]{0,2,1:T(8,128)}) %reduce-scatter.9.cloned.1.call-update) | async-done | bytes 1048592 | tf_op jit(solution)/shard_map/reduce_scatter | solution.py:246
  372.0 1.9 reduce.6
  373.9 2.3 copy.130
  376.2 2.0 reshape.506
  378.2 4.6 all-to-all-start.3
  382.8 130.3 %all-gather.14.cloned.1.call-done = bf16[2048,4096]{1,0:T(8,128)(2,1)} async-done(((bf16[128,4096]{1,0:T(8,128)(2,1)}), bf16[2048,4096]{1,0:T(8,128)(2,1)}) %all-gather.14.cloned.1.call-update) | async-done | bytes 16777232 | tf_op jit(solution)/shard_map/all_gather | solution.py:102
  513.1 10.6 fusion.133
  523.7 12.7 fusion.73
  536.4 3.7 reshape.507
  540.1 2.4 copy.112
  542.6 2.3 copy.106
  544.9 10.1 fusion.134
  555.1 1.8 reduce.5
  557.6 12.9 all_to_all.67
  571.5 1.8 copy.111
  574.4 12.5 fusion.129
  586.9 5.0 convolution_add_fusion.2
  592.0 1.4 convert_reduce_fusion
  594.0 22.4 %all-reduce.7.cloned.1.call-done = (f32[128,2048]{1,0:T(8,128)}, f32[128,2048]{1,0:T(8,128)}) async-done(((f32[128,2048]{1,0:T(8,128)}, f32[128,2048]{1,0:T(8,128)}), (f32[128,2048]{1,0:T(8,128)}, f32[128,2048]{1,0:T(8,128)})) %all-reduce.7.cloned.1.call-update) | async-done | bytes 2097168 | tf_op jit(solution)/shard_map/psum | solution.py:262
  616.3 3.0 fusion.130
  619.4 1.5 convert_reduce_fusion.2
  621.0 4.5 convolution_bitcast_fusion.4
  625.6 13.3 convolution_bitcast_fusion.3
  640.0 10.2 fusion.128
  651.4 13.3 fusion.71
  665.7 1.8 add_convert_fusion.2
  667.5 65.7 %all-reduce.5.cloned.1.call-done = (f32[2048]{0:T(1024)}, f32[2048]{0:T(1024)}, f32[2048]{0:T(1024)}, f32[2048]{0:T(1024)}, f32[3072]{0:T(1024)}, /*index=5*/f32[1024]{0:T(1024)}, f32[4096]{0:T(1024)}) async-done(((f32[2048]{0:T(1024)}, f32[2048]{0:T(1024)}, f32[2048]{0:T(1024)}, f32[2048]{0:T(1024)}, f32[3072]{0:T(1024)}, /*index=5*/f32[1024]{0:T(1024)}, f32[4096]{0:T(1024)}), (f32[2048]{0:T(1024)}, ...) | async-done | bytes 65552 | tf_op jit(solution)/shard_map/psum | solution.py:292
  733.2 109.3 %reduce-scatter.13.cloned.1.call-done = f32[128,1024]{0,1:T(8,128)} async-done(((f32[2048,1024]{0,1:T(8,128)}), f32[128,1024]{0,1:T(8,128)}) %reduce-scatter.13.cloned.1.call-update) | async-done | bytes 524304 | tf_op jit(solution)/shard_map/reduce_scatter | solution.py:280
  842.5 2.0 copy.107
  844.6 332.1 %reduce-scatter.17.cloned.1.call-done = f32[128,4096]{0,1:T(8,128)} async-done(((f32[2048,4096]{0,1:T(8,128)}), f32[128,4096]{0,1:T(8,128)}) %reduce-scatter.17.cloned.1.call-update) | async-done | bytes 2097168 | tf_op jit(solution)/shard_map/reduce_scatter | solution.py:282
  1176.7 2.9 copy.108
  1179.6 244.3 %reduce-scatter.11.cloned.1.call-done = f32[128,3072]{1,0:T(8,128)} async-done(((f32[2048,3072]{1,0:T(8,128)}), f32[128,3072]{1,0:T(8,128)}) %reduce-scatter.11.cloned.1.call-update) | async-done | bytes 1572880 | tf_op jit(solution)/shard_map/reduce_scatter | solution.py:279
  1423.9 334.5 %reduce-scatter.15.cloned.1.call-done = f32[128,4096]{1,0:T(8,128)} async-done(((f32[2048,4096]{1,0:T(8,128)}), f32[128,4096]{1,0:T(8,128)}) %reduce-scatter.15.cloned.1.call-update) | async-done | bytes 2097168 | tf_op jit(solution)/shard_map/reduce_scatter | solution.py:281
  (175 shorter events, 34.0 us)
Async XLA Ops:
  7.2 106.3 %copy-start.16 = (f32[2048]{0:T(1024)S(1)}, f32[2048]{0:T(1024)}, u32[]{:S(2)}) copy-start(f32[2048]{0:T(1024)} %param.20) | copy-start | bytes 24580
  7.2 106.3 %copy-start.17 = (f32[2048]{0:T(1024)S(1)}, f32[2048]{0:T(1024)}, u32[]{:S(2)}) copy-start(f32[2048]{0:T(1024)} %param.21) | copy-start | bytes 24580
  7.2 106.3 %copy-start.21 = (f32[3072]{0:T(1024)S(1)}, f32[3072]{0:T(1024)}, u32[]{:S(2)}) copy-start(f32[3072]{0:T(1024)} %param.25) | copy-start | bytes 36868
  7.2 106.3 %all-gather.6.cloned.1.call-start = ((), (), s32[]{:S(2)}) async-start(), calls=%async_computation.10 | async-start | bytes 13369344 | tf_op jit(solution)/shard_map/all_gather | solution.py:99
  7.9 162.4 %all-gather.10.cloned.1.call-start = ((), (), s32[]{:S(2)}) async-start(), calls=%async_computation.12 | async-start | bytes 4456448 | tf_op jit(solution)/shard_map/all_gather | solution.py:100
  8.7 185.7 %all-gather.8.cloned.1.call-start = ((), (), s32[]{:S(2)}) async-start(), calls=%async_computation.11 | async-start | bytes 2621440 | tf_op jit(solution)/shard_map/all_gather | solution.py:126
  19.0 101.1 %copy-start = (bf16[128,2048]{1,0:T(8,128)(2,1)}, bf16[128,2048]{1,0:T(8,128)(2,1)S(1)}, u32[]{:S(2)}) copy-start(bf16[128,2048]{1,0:T(8,128)(2,1)S(1)} %all_gather.26) | copy-start | bytes 1572868
  125.7 35.1 %copy-start.11 = (bf16[128,1024]{1,0:T(8,128)(2,1)S(1)}, bf16[128,1024]{1,0:T(8,128)(2,1)}, u32[]{:S(2)}) copy-start(bf16[128,1024]{1,0:T(8,128)(2,1)} %param.19) | copy-start | bytes 786436
  160.2 162.6 %all-gather.12.cloned.1.call-start = ((), (), s32[]{:S(2)}) async-start(), calls=%async_computation.13 | async-start | bytes 17825792 | tf_op jit(solution)/shard_map/all_gather | solution.py:101
  169.0 4.3 copy-start.7
  174.0 31.7 %all-to-all-start.2 = ((bf16[128,4,256]{2,0,1:T(8,128)(2,1)}), bf16[128,4,256]{2,0,1:T(8,128)(2,1)S(1)}, u32[]{:S(2)}, u32[]{:S(2)}) async-start(bf16[128,4,256]{2,0,1:T(8,128)(2,1)} %bitcast.160), calls=%async_computation.3 | async-start | bytes 524288 | tf_op jit(solution)/shard_map/all_to_all | solution.py:198
  177.4 190.4 %reduce-scatter.9.cloned.1.call-start = ((), (), s32[]{:S(2)}) async-start(), calls=%async_computation.16 | async-start | bytes 5242880 | tf_op jit(solution)/shard_map/reduce_scatter | solution.py:246
  206.6 1.3 copy-start.5
  215.2 3.2 copy-start.2
  218.3 2.4 copy-start.6
  219.9 0.8 copy-start.3
  220.7 1.3 copy-start.5
  229.2 3.2 copy-start.2
  232.4 2.4 copy-start.6
  234.0 0.8 copy-start.3
  240.3 11.0 copy-start.4
  240.3 82.6 %copy-start.1 = (bf16[128,2048]{1,0:T(8,128)(2,1)S(1)}, bf16[128,2048]{1,0:T(8,128)(2,1)}, u32[]{:S(2)}) copy-start(bf16[128,2048]{1,0:T(8,128)(2,1)} %copy-done) | copy-start | bytes 1572868
  240.3 82.6 %copy-start.14 = (f32[2048]{0:T(1024)S(1)}, f32[2048]{0:T(1024)}, u32[]{:S(2)}) copy-start(f32[2048]{0:T(1024)} %param.22) | copy-start | bytes 24580
  240.3 82.6 %copy-start.15 = (f32[2048]{0:T(1024)S(1)}, f32[2048]{0:T(1024)}, u32[]{:S(2)}) copy-start(f32[2048]{0:T(1024)} %param.23) | copy-start | bytes 24580
  240.3 82.6 %copy-start.18 = (f32[4096]{0:T(1024)S(1)}, f32[4096]{0:T(1024)}, u32[]{:S(2)}) copy-start(f32[4096]{0:T(1024)} %param.29) | copy-start | bytes 49156
  240.3 272.8 %all-gather.14.cloned.1.call-start = ((), (), s32[]{:S(2)}) async-start(), calls=%async_computation.14 | async-start | bytes 17825792 | tf_op jit(solution)/shard_map/all_gather | solution.py:102
  373.9 139.2 %copy-start.8 = (bf16[128,2048]{1,0:T(8,128)(2,1)S(1)}, bf16[128,2048]{1,0:T(8,128)(2,1)}, u32[]{:S(2)}) copy-start(bf16[128,2048]{1,0:T(8,128)(2,1)} %copy-done.7) | copy-start | bytes 1572868
  378.2 158.1 %all-to-all-start.3 = ((bf16[4,2,49152]{2,1,0:T(2,128)(2,1)}), bf16[4,2,49152]{2,1,0:T(2,128)(2,1)}, u32[]{:S(2)}, u32[]{:S(2)}) async-start(bf16[4,2,49152]{2,1,0:T(2,128)(2,1)} %reshape.506), calls=%async_computation.5 | async-start | bytes 1572864 | tf_op jit(solution)/shard_map/all_to_all | solution.py:256
  382.8 233.5 %all-reduce.7.cloned.1.call-start = ((), (), s32[]{:S(2)}) async-start(), calls=%async_computation.22 | async-start | bytes 4194304 | tf_op jit(solution)/shard_map/psum | solution.py:262
  555.0 109.8 %reduce-scatter.7.cloned.1.call-start = ((), (), s32[]{:S(2)}) async-start(), calls=%async_computation.15 | async-start | bytes 1572864 | tf_op jit(solution)/shard_map/reduce_scatter | solution.py:182
  591.9 141.3 %all-reduce.5.cloned.1.call-start = ((), (), s32[]{:S(2)}) async-start(), calls=%async_computation.21 | async-start | bytes 131072 | tf_op jit(solution)/shard_map/psum | solution.py:292
  616.3 3.0 copy-start.12
  620.9 221.6 %reduce-scatter.13.cloned.1.call-start = ((), (), s32[]{:S(2)}) async-start(), calls=%async_computation.18 | async-start | bytes 8912896 | tf_op jit(solution)/shard_map/reduce_scatter | solution.py:280
  625.5 551.2 %reduce-scatter.17.cloned.1.call-start = ((), (), s32[]{:S(2)}) async-start(), calls=%async_computation.20 | async-start | bytes 35651584 | tf_op jit(solution)/shard_map/reduce_scatter | solution.py:282
  638.8 1.1 copy-start.9
  638.9 785.0 %reduce-scatter.11.cloned.1.call-start = ((), (), s32[]{:S(2)}) async-start(), calls=%async_computation.17 | async-start | bytes 26738688 | tf_op jit(solution)/shard_map/reduce_scatter | solution.py:279
  650.2 1.2 copy-start.10
  650.2 1108.2 %reduce-scatter.15.cloned.1.call-start = ((), (), s32[]{:S(2)}) async-start(), calls=%async_computation.19 | async-start | bytes 35651584 | tf_op jit(solution)/shard_map/reduce_scatter | solution.py:281
  664.7 1.0 copy-start.13
  664.7 1.0 copy-start.27
  664.8 1.0 copy-start.28
  844.5 913.9 %copy-start.20 = (f32[1024]{0:T(1024)S(1)}, f32[1024]{0:T(1024)}, u32[]{:S(2)}) copy-start(f32[1024]{0:T(1024)} %get-tuple-element.611) | copy-start | bytes 12292
  844.5 914.5 %copy-start.26 = (f32[2048]{0:T(1024)S(1)}, f32[2048]{0:T(1024)}, u32[]{:S(2)}) copy-start(f32[2048]{0:T(1024)} %get-tuple-element.604) | copy-start | bytes 24580
  844.5 915.1 %copy-start.25 = (f32[2048]{0:T(1024)S(1)}, f32[2048]{0:T(1024)}, u32[]{:S(2)}) copy-start(f32[2048]{0:T(1024)} %get-tuple-element.605) | copy-start | bytes 24580
  844.5 915.7 %copy-start.24 = (f32[2048]{0:T(1024)S(1)}, f32[2048]{0:T(1024)}, u32[]{:S(2)}) copy-start(f32[2048]{0:T(1024)} %get-tuple-element.606) | copy-start | bytes 24580
  844.5 916.3 %copy-start.23 = (f32[2048]{0:T(1024)S(1)}, f32[2048]{0:T(1024)}, u32[]{:S(2)}) copy-start(f32[2048]{0:T(1024)} %get-tuple-element.607) | copy-start | bytes 24580
  844.5 916.9 %copy-start.22 = (f32[3072]{0:T(1024)S(1)}, f32[3072]{0:T(1024)}, u32[]{:S(2)}) copy-start(f32[3072]{0:T(1024)} %get-tuple-element.609) | copy-start | bytes 36868
  844.5 918.1 %copy-start.19 = (f32[4096]{0:T(1024)S(1)}, f32[4096]{0:T(1024)}, u32[]{:S(2)}) copy-start(f32[4096]{0:T(1024)} %get-tuple-element.613) | copy-start | bytes 49156
Sparse Core Ops, SparseCore 0:
  10.3 103.1 all-gather.5
  115.7 54.6 all-gather.9
  172.5 21.8 all-gather.7
  196.4 126.4 all-gather.11
  325.2 42.5 reduce-scatter.8
  369.9 143.1 all-gather.13
  555.2 61.1 all-reduce.6
  619.2 20.3 reduce-scatter.6
  645.2 87.9 all-reduce.4
  737.1 105.3 reduce-scatter.12
  846.7 329.9 reduce-scatter.16
  1181.2 242.6 reduce-scatter.10
  1428.7 329.6 reduce-scatter.14
where the time goes:
time: 1780 us; the launch traced here: 1770 us
  waiting for transfers between devices  1460 us (82%)
  matrix products  131 us (7%)
  blocking collectives  64.9 us (4%)
  local copies, waits for them, and re-layouts  59.3 us (3%)
  starting transfers between devices  19.6 us (1%)
    reduce_scatter x1, waiting for transfers between devices, per_device(): lax.psum_scatter(up_term, ('seq', 'fsdp'), scatter_dimension=0, tiled=True)  335 us
    reduce_scatter x1, waiting for transfers between devices, per_device(): lax.psum_scatter(down_term, ('seq', 'fsdp'), scatter_dimension=0, tiled=T...  332 us
    reduce_scatter x1, waiting for transfers between devices, per_device(): lax.psum_scatter(qkv_term, ('seq', 'fsdp'), scatter_dimension=0, tiled=True)  244 us
    all_gather x1, waiting for transfers between devices, per_device(): lax.all_gather(down_weight, ('seq', 'fsdp'), axis=0, tiled=True)  130 us
    reduce_scatter x1, waiting for transfers between devices, per_device(): lax.psum_scatter(proj_term, ('seq', 'fsdp'), scatter_dimension=0, tiled=T...  109 us
    all_gather x1, waiting for transfers between devices, per_device(): lax.all_gather(qkv_weight, ('seq', 'fsdp'), axis=0, tiled=True)  93.9 us
    all_gather x1, waiting for transfers between devices, per_device(): lax.all_gather(up_weight, ('seq', 'fsdp'), axis=0, tiled=True)  70.9 us
    psum x1, waiting for transfers between devices, per_device(): lax.psum((qkv_bias_term, out_bias_term, up_bias_term, attn_gain_term, att...  65.7 us
  transfers between devices with their start and end apart: 15, of which 12 were waited for; matrix products, arithmetic and copies ran while one was open for 10% of the time, Pallas kernels for 0%

commit v1 on v0

--- a/solution.py
+++ b/solution.py
@@ -8,6 +8,22 @@
 ROT = 64
 norm_eps = 1e-05
 rope_base = 10000.0
+
+
+def ring_gather(x, axis, dim):
+    ways, here, step = (lax.axis_size(axis), lax.axis_index(axis), x.shape[dim])
+    shape = [n * ways if d == dim else n for d, n in enumerate(x.shape)]
+    full = lax.dynamic_update_slice_in_dim(jnp.zeros(shape, x.dtype), x, here * step, axis=dim)
+    going_up = going_down = x
+    for far in range(1, ways // 2 + 1):
+        going_up = lax.ppermute(going_up, axis, [(d, (d + 1) % ways) for d in range(ways)])
+        full = lax.dynamic_update_slice_in_dim(full, going_up, (here - far) % ways * step, axis=dim)
+        if 2 * far < ways:
+            going_down = lax.ppermute(going_down, axis, [(d, (d - 1) % ways) for d in range(ways)])
+            full = lax.dynamic_update_slice_in_dim(
+                full, going_down, (here + far) % ways * step, axis=dim
+            )
+    return full
 
 
 def gelu_value(pre_act):
@@ -96,7 +112,7 @@
     attn_in = (normal_rows * attn_norm_gain + attn_norm_bias).astype(jnp.bfloat16)
     mlp_in = (normal_rows * mlp_norm_gain + mlp_norm_bias).astype(jnp.bfloat16)
     qkv_full, proj_full, up_full, down_full = (
-        lax.all_gather(qkv_weight, ("seq", "fsdp"), axis=0, tiled=True),
+        ring_gather(qkv_weight, ("seq", "fsdp"), 0),
         lax.all_gather(proj_weight, ("seq", "fsdp"), axis=0, tiled=True),
         lax.all_gather(up_weight, ("seq", "fsdp"), axis=0, tiled=True),
         lax.all_gather(down_weight, ("seq", "fsdp"), axis=0, tiled=True),

time: 1780 us -> 1930 us (1.084)
  starting transfers between devices: 19.6 us -> 76.2 us
  waiting for transfers between devices: 1460 us -> 1510 us
  blocking collectives: 64.9 us -> 91.1 us
    ppermute x0 -> x15, starting transfers between devices: none -> 71.7 us  [the longest x8 53.8 us: ring_gather(): lax.ppermute(going_up, axis, [(d, (d + 1) % ways) for d in range(ways)])]
    reduce_scatter x1, waiting for transfers between devices: 109 us -> 60.7 us  [per_device(): lax.psum_scatter(proj_term, ('seq', 'fsdp'), scatter_dimension=0, tiled=T...]
    ppermute x0 -> x15, waiting for transfers between devices: none -> 48.1 us  [the longest x8 24.5 us: ring_gather(): lax.ppermute(going_up, axis, [(d, (d + 1) % ways) for d in range(ways)])]
    all_gather x1, waiting for transfers between devices: 70.9 us -> 117 us  [per_device(): lax.all_gather(up_weight, ('seq', 'fsdp'), axis=0, tiled=True)]
    all_to_all x0 -> x1, blocking collectives: none -> 44.3 us  [per_device(): lax.all_to_all(grads_packed, 'seq', split_axis=0, concat_axis=1, tiled=True)]
    all_gather x1, waiting for transfers between devices: 93.9 us -> 63.2 us  [per_device(): lax.all_gather(qkv_weight, ('seq', 'fsdp'), axis=0, tiled=True)]
    psum x1, waiting for transfers between devices: 65.7 us -> 91.6 us  [per_device(): lax.psum((qkv_bias_term, out_bias_term, up_bias_term, attn_gain_term, att...]
    reduce_scatter x1, waiting for transfers between devices: 0.02 us -> 20.8 us  [per_device(): lax.psum_scatter(attn_branch + mlp_branch, 'tensor', scatter_dimension=1,...]
  transfers between devices with their start and end apart: 15 -> 29, of which waited for: 12 -> 21; matrix products, arithmetic and copies ran while one was open for 10% -> 9% of each run, Pallas kernels for 0% -> 0%
where the time goes in v1:
time: 1930 us; the launch traced here: 1920 us
  waiting for transfers between devices  1510 us (78%)
  matrix products  134 us (7%)
  blocking collectives  91.1 us (5%)
  local copies, waits for them, and re-layouts  76.3 us (4%)
  starting transfers between devices  76.2 us (4%)
    reduce_scatter x1, waiting for transfers between devices, per_device(): lax.psum_scatter(down_term, ('seq', 'fsdp'), scatter_dimension=0, tiled=T...  336 us
    reduce_scatter x1, waiting for transfers between devices, per_device(): lax.psum_scatter(up_term, ('seq', 'fsdp'), scatter_dimension=0, tiled=True)  334 us
    reduce_scatter x1, waiting for transfers between devices, per_device(): lax.psum_scatter(qkv_term, ('seq', 'fsdp'), scatter_dimension=0, tiled=True)  244 us
    all_gather x1, waiting for transfers between devices, per_device(): lax.all_gather(down_weight, ('seq', 'fsdp'), axis=0, tiled=True)  118 us
    all_gather x1, waiting for transfers between devices, per_device(): lax.all_gather(up_weight, ('seq', 'fsdp'), axis=0, tiled=True)  117 us
    psum x1, waiting for transfers between devices, per_device(): lax.psum((qkv_bias_term, out_bias_term, up_bias_term, attn_gain_term, att...  91.6 us
    all_gather x1, waiting for transfers between devices, per_device(): lax.all_gather(qkv_weight, ('seq', 'fsdp'), axis=0, tiled=True)  63.2 us
    reduce_scatter x1, waiting for transfers between devices, per_device(): lax.psum_scatter(proj_term, ('seq', 'fsdp'), scatter_dimension=0, tiled=T...  60.7 us
  transfers between devices with their start and end apart: 29, of which 21 were waited for; matrix products, arithmetic and copies ran while one was open for 9% of the time, Pallas kernels for 0%

profile of v1, /device:TPU:0, one launch (start us, length us, event | category | flops | bytes accessed | tf_op | source)
XLA Modules:
  0.0 1921.5 jit_solution(1101132286604750451)
XLA Ops:
  7.8 5.0 collective-permute-start.1
  12.8 9.9 collective-permute-done
  22.7 5.3 collective-permute-start.2
  28.1 8.7 all_gather.25
  37.0 2.3 collective-permute-start.4
  39.6 6.1 broadcast_in_dim.33
  46.7 7.9 collective-permute-done.3
  54.6 4.8 collective-permute-start.5
  62.0 15.6 collective-permute-done.5
  77.6 4.6 collective-permute-start.7
  84.1 11.9 collective-permute-start.8
  96.9 2.1 constant_dynamic-update-slice_fusion.12
  99.1 3.4 collective-permute-start.9
  102.5 2.1 constant_dynamic-update-slice_fusion.11
  104.5 4.5 collective-permute-done.8
  109.0 7.1 collective-permute-start.10
  116.2 2.1 constant_dynamic-update-slice_fusion.10
  118.2 2.1 constant_dynamic-update-slice_fusion.9
  121.3 2.6 collective-permute-done.10
  123.9 12.0 collective-permute-start.12
  138.8 3.7 collective-permute-done.12
  142.4 13.3 collective-permute-start.14
  158.6 2.8 collective-permute-done.14
  162.3 6.5 convolution_add_fusion.1
  174.5 18.1 all_to_all.66
  193.6 7.0 all_gather.30
  200.7 3.1 convolution_convert_fusion
  204.5 3.4 all-to-all-start.2
  208.5 13.1 all-gather.6.cloned.1.call-done
  221.5 11.1 while.28
  225.0 2.0 fusion.179
  230.5 2.0 fusion.179
  233.7 28.1 %while.29 = (s32[]{:T(128)}, f32[512,1,256]{0,2,1:T(8,128)}, f32[2,1024,1,512]{3,1,0,2:T(8,128)}, s32[2]{0:T(128)S(1)}, bf16[2048,1,512]{2,0,1:T(8,128)(2,1)}, /...) while((s32[]{:T(128)}, f32[512,1,256]{0,2,1:T(8,128)}, ...), condition=%wide.region_9.10_spmd.clone, body=%wide.region_8.9_spmd.clone.sunk | while | flops 1347952640 | bytes 34100076 | solution.py:260
  242.2 3.2 constant_dynamic-update-slice_fusion.18
  256.3 3.1 constant_dynamic-update-slice_fusion.18
  261.8 5.4 copy.104
  269.8 42.0 %reduce-scatter.9.cloned.1.call-done = f32[512,1,512]{0,2,1:T(8,128)} async-done(((f32[2048,1,512]{0,2,1:T(8,128)}), f32[512,1,512]{0,2,1:T(8,128)}) %reduce-scatter.9.cloned.1.call-update) | async-done | bytes 1048592 | tf_op jit(solution)/shard_map/reduce_scatter | solution.py:262
  317.8 44.3 %all_to_all.67 = bf16[4,2,49152]{2,1,0:T(2,128)(2,1)S(1)} all-to-all(bf16[4,2,49152]{2,1,0:T(2,128)(2,1)S(1)} %reshape.506), channel_id=1, replica_groups=mesh['seq'=4,'tensor'=2,'fsdp'=4] {'seq'}, dimensions={0} | all-to-all | bytes 1572864 | tf_op jit(solution)/shard_map/all_to_all | solution.py:272
  362.1 2.2 reshape.507
  366.2 63.2 %all-gather.14.cloned.1.call-done = bf16[2048,3072]{1,0:T(8,128)(2,1)} async-done(((bf16[128,3072]{1,0:T(8,128)(2,1)}), bf16[2048,3072]{1,0:T(8,128)(2,1)}) %all-gather.14.cloned.1.call-update) | async-done | bytes 12582928 | tf_op jit(solution)/shard_map/all_gather | solution.py:205
  429.4 9.9 fusion.134
  439.3 116.8 %all-gather.10.cloned.1.call-done = bf16[2048,4096]{1,0:T(8,128)(2,1)} async-done(((bf16[128,4096]{1,0:T(8,128)(2,1)}), bf16[2048,4096]{1,0:T(8,128)(2,1)}) %all-gather.10.cloned.1.call-update) | async-done | bytes 16777232 | tf_op jit(solution)/shard_map/all_gather | solution.py:117
  556.1 8.2 convolution_add_fusion
  564.4 118.4 %all-gather.12.cloned.1.call-done = bf16[2048,4096]{1,0:T(8,128)(2,1)} async-done(((bf16[128,4096]{1,0:T(8,128)(2,1)}), bf16[2048,4096]{1,0:T(8,128)(2,1)}) %all-gather.12.cloned.1.call-update) | async-done | bytes 16777232 | tf_op jit(solution)/shard_map/all_gather | solution.py:118
  682.8 10.5 fusion.133
  693.3 12.9 fusion.73
  708.9 12.9 all_to_all.68
  725.7 4.5 convolution_bitcast_fusion.4
  730.3 12.4 fusion.129
  742.8 5.5 convolution_add_fusion.2
  750.2 17.4 all-reduce.7.cloned.1.call-done
  767.6 3.0 fusion.130
  772.2 16.0 convolution_bitcast_fusion.3
  789.5 10.6 fusion.128
  801.3 13.3 fusion.71
  814.6 60.7 %reduce-scatter.13.cloned.1.call-done = f32[128,1024]{0,1:T(8,128)} async-done(((f32[2048,1024]{0,1:T(8,128)}), f32[128,1024]{0,1:T(8,128)}) %reduce-scatter.13.cloned.1.call-update) | async-done | bytes 524304 | tf_op jit(solution)/shard_map/reduce_scatter | solution.py:296
  875.3 2.0 copy.107
  877.3 20.8 %reduce-scatter.7.cloned.1.call-done = f32[128,1024]{1,0:T(8,128)} async-done(((f32[128,2048]{1,0:T(8,128)}), f32[128,1024]{1,0:T(8,128)}) %reduce-scatter.7.cloned.1.call-update) | async-done | bytes 524304 | tf_op jit(solution)/shard_map/reduce_scatter | solution.py:198
  898.2 1.8 add_convert_fusion.2
  900.0 91.6 %all-reduce.5.cloned.1.call-done = (f32[2048]{0:T(1024)}, f32[2048]{0:T(1024)}, f32[2048]{0:T(1024)}, f32[2048]{0:T(1024)}, f32[3072]{0:T(1024)}, /*index=5*/f32[1024]{0:T(1024)}, f32[4096]{0:T(1024)}) async-done(((f32[2048]{0:T(1024)}, f32[2048]{0:T(1024)}, f32[2048]{0:T(1024)}, f32[2048]{0:T(1024)}, f32[3072]{0:T(1024)}, /*index=5*/f32[1024]{0:T(1024)}, f32[4096]{0:T(1024)}), (f32[2048]{0:T(1024)}, ...) | async-done | bytes 65552 | tf_op jit(solution)/shard_map/psum | solution.py:308
  991.7 336.4 %reduce-scatter.17.cloned.1.call-done = f32[128,4096]{0,1:T(8,128)} async-done(((f32[2048,4096]{0,1:T(8,128)}), f32[128,4096]{0,1:T(8,128)}) %reduce-scatter.17.cloned.1.call-update) | async-done | bytes 2097168 | tf_op jit(solution)/shard_map/reduce_scatter | solution.py:298
  1328.0 2.9 copy.108
  1330.9 244.3 %reduce-scatter.11.cloned.1.call-done = f32[128,3072]{1,0:T(8,128)} async-done(((f32[2048,3072]{1,0:T(8,128)}), f32[128,3072]{1,0:T(8,128)}) %reduce-scatter.11.cloned.1.call-update) | async-done | bytes 1572880 | tf_op jit(solution)/shard_map/reduce_scatter | solution.py:295
  1575.3 334.5 %reduce-scatter.15.cloned.1.call-done = f32[128,4096]{1,0:T(8,128)} async-done(((f32[2048,4096]{1,0:T(8,128)}), f32[128,4096]{1,0:T(8,128)}) %reduce-scatter.15.cloned.1.call-update) | async-done | bytes 2097168 | tf_op jit(solution)/shard_map/reduce_scatter | solution.py:297
  (227 shorter events, 77.5 us)
Async XLA Ops:
  7.2 193.5 %all-gather.8.cloned.1.call-start = ((), (), s32[]{:S(2)}) async-start(), calls=%async_computation.11 | async-start | bytes 4456448 | tf_op jit(solution)/shard_map/all_gather | solution.py:116
  7.2 15.5 collective-permute-start
  7.8 29.2 %collective-permute-start.1 = (bf16[128,3072]{1,0:T(8,128)(2,1)}, bf16[128,3072]{1,0:T(8,128)(2,1)S(1)}, u32[]{:S(2)}, u32[]{:S(2)}) collective-permute-start(bf16[128,3072]{1,0:T(8,128)(2,1)} %param.24), channel_id=1, source_target_pairs={{0,27},{1,0},{2,1},{3,2},{8,3},{9,8},{10,9},{11,10},{16,11},{17,16... | collective-permute-start | bytes 2359304 | tf_op jit(solution)/shard_map/ppermute | solution.py:22
  22.7 14.3 collective-permute-start.2
  28.1 193.5 %all-gather.6.cloned.1.call-start = ((), (), s32[]{:S(2)}) async-start(), calls=%async_computation.10 | async-start | bytes 2621440 | tf_op jit(solution)/shard_map/all_gather | solution.py:142
  36.8 125.5 %copy-start = (bf16[128,2048]{1,0:T(8,128)(2,1)}, bf16[128,2048]{1,0:T(8,128)(2,1)S(1)}, u32[]{:S(2)}) copy-start(bf16[128,2048]{1,0:T(8,128)(2,1)S(1)} %all_gather.25) | copy-start | bytes 1572868
  36.9 17.6 collective-permute-start.3
  37.0 22.7 %collective-permute-start.4 = (bf16[128,3072]{1,0:T(8,128)(2,1)S(1)}, bf16[128,3072]{1,0:T(8,128)(2,1)}, u32[]{:S(2)}, u32[]{:S(2)}) collective-permute-start(bf16[128,3072]{1,0:T(8,128)(2,1)S(1)} %collective-permute-done.2), channel_id=1, source_target_pairs={{0,1},{1,2},{2,3},{3,8},{8,9},{9,10},{10,11},{11,16},{16,17},{17,1... | collective-permute-start | bytes 2359304 | tf_op jit(solution)/shard_map/ppermute | solution.py:19
  39.6 6.1 copy-start.13
  54.6 23.0 %collective-permute-start.5 = (bf16[128,3072]{1,0:T(8,128)(2,1)}, bf16[128,3072]{1,0:T(8,128)(2,1)}, u32[]{:S(2)}, u32[]{:S(2)}) collective-permute-start(bf16[128,3072]{1,0:T(8,128)(2,1)} %collective-permute-done.3), channel_id=1, source_target_pairs={{0,27},{1,0},{2,1},{3,2},{8,3},{9,8},{10,9},{11,10},{16,11},{17,16... | collective-permute-start | bytes 2359304 | tf_op jit(solution)/shard_map/ppermute | solution.py:22
  59.7 24.3 %collective-permute-start.6 = (bf16[128,3072]{1,0:T(8,128)(2,1)}, bf16[128,3072]{1,0:T(8,128)(2,1)}, u32[]{:S(2)}, u32[]{:S(2)}) collective-permute-start(bf16[128,3072]{1,0:T(8,128)(2,1)} %collective-permute-done.4), channel_id=1, source_target_pairs={{0,1},{1,2},{2,3},{3,8},{8,9},{9,10},{10,11},{11,16},{16,17},{17,1... | collective-permute-start | bytes 2359304 | tf_op jit(solution)/shard_map/ppermute | solution.py:19
  77.6 21.5 %collective-permute-start.7 = (bf16[128,3072]{1,0:T(8,128)(2,1)}, bf16[128,3072]{1,0:T(8,128)(2,1)S(1)}, u32[]{:S(2)}, u32[]{:S(2)}) collective-permute-start(bf16[128,3072]{1,0:T(8,128)(2,1)} %collective-permute-done.5), channel_id=1, source_target_pairs={{0,27},{1,0},{2,1},{3,2},{8,3},{9,8},{10,9},{11,10},{16,11},{17,16... | collective-permute-start | bytes 2359304 | tf_op jit(solution)/shard_map/ppermute | solution.py:22
  84.1 24.9 %collective-permute-start.8 = (bf16[128,3072]{1,0:T(8,128)(2,1)}, bf16[128,3072]{1,0:T(8,128)(2,1)S(1)}, u32[]{:S(2)}, u32[]{:S(2)}) collective-permute-start(bf16[128,3072]{1,0:T(8,128)(2,1)} %collective-permute-done.6), channel_id=1, source_target_pairs={{0,1},{1,2},{2,3},{3,8},{8,9},{9,10},{10,11},{11,16},{16,17},{17,1... | collective-permute-start | bytes 2359304 | tf_op jit(solution)/shard_map/ppermute | solution.py:19
  99.1 21.2 %collective-permute-start.9 = (bf16[128,3072]{1,0:T(8,128)(2,1)S(1)}, bf16[128,3072]{1,0:T(8,128)(2,1)S(1)}, u32[]{:S(2)}, u32[]{:S(2)}) collective-permute-start(bf16[128,3072]{1,0:T(8,128)(2,1)S(1)} %collective-permute-done.7), channel_id=1, source_target_pairs={{0,27},{1,0},{2,1},{3,2},{8,3},{9,8},{10,9},{11,10},{16,11},{17,16... | collective-permute-start | bytes 2359304 | tf_op jit(solution)/shard_map/ppermute | solution.py:22
  109.0 14.8 collective-permute-start.10
  120.3 17.5 collective-permute-start.11
  123.9 18.6 collective-permute-start.12
  137.8 19.9 %collective-permute-start.13 = (bf16[128,3072]{1,0:T(8,128)(2,1)S(1)}, bf16[128,3072]{1,0:T(8,128)(2,1)S(1)}, u32[]{:S(2)}, u32[]{:S(2)}) collective-permute-start(bf16[128,3072]{1,0:T(8,128)(2,1)S(1)} %collective-permute-done.11), channel_id=1, source_target_pairs={{0,27},{1,0},{2,1},{3,2},{8,3},{9,8},{10,9},{11,10},{16,11},{17,16... | collective-permute-start | bytes 2359304 | tf_op jit(solution)/shard_map/ppermute | solution.py:22
  142.4 18.9 collective-permute-start.14
  156.7 5.6 copy-start.19
  156.7 5.6 copy-start.20
  156.7 5.6 copy-start.24
  174.5 19.0 copy-start.14
  200.6 3.1 copy-start.7
  204.5 28.4 %all-to-all-start.2 = ((bf16[128,4,256]{2,0,1:T(8,128)(2,1)}), bf16[128,4,256]{2,0,1:T(8,128)(2,1)S(1)}, u32[]{:S(2)}, u32[]{:S(2)}) async-start(bf16[128,4,256]{2,0,1:T(8,128)(2,1)} %bitcast.160), calls=%async_computation.3 | async-start | bytes 524288 | tf_op jit(solution)/shard_map/all_to_all | solution.py:214
  207.9 104.0 %reduce-scatter.9.cloned.1.call-start = ((), (), s32[]{:S(2)}) async-start(), calls=%async_computation.15 | async-start | bytes 5242880 | tf_op jit(solution)/shard_map/reduce_scatter | solution.py:262
  233.7 1.3 copy-start.5
  242.2 3.2 copy-start.2
  245.4 2.4 copy-start.6
  247.0 0.8 copy-start.3
  247.8 1.3 copy-start.5
  256.3 3.1 copy-start.2
  259.5 2.4 copy-start.6
  267.3 1.8 copy-start.4
  267.3 162.1 %all-gather.14.cloned.1.call-start = ((), (), s32[]{:S(2)}) async-start(), calls=%async_computation.16 | async-start | bytes 13369344 | tf_op jit(solution)/shard_map/all_gather | solution.py:205
  267.9 288.2 %all-gather.10.cloned.1.call-start = ((), (), s32[]{:S(2)}) async-start(), calls=%async_computation.12 | async-start | bytes 17825792 | tf_op jit(solution)/shard_map/all_gather | solution.py:117
  268.5 414.3 %all-gather.12.cloned.1.call-start = ((), (), s32[]{:S(2)}) async-start(), calls=%async_computation.13 | async-start | bytes 17825792 | tf_op jit(solution)/shard_map/all_gather | solution.py:118
  269.1 498.6 %all-reduce.7.cloned.1.call-start = ((), (), s32[]{:S(2)}) async-start(), calls=%async_computation.22 | async-start | bytes 4194304 | tf_op jit(solution)/shard_map/psum | solution.py:278
  365.8 73.5 %copy-start.11 = (bf16[512,1,768]{2,0,1:T(8,128)(2,1)}, bf16[512,1,768]{2,0,1:T(8,128)(2,1)S(1)}, u32[]{:S(2)}) copy-start(bf16[512,1,768]{2,0,1:T(8,128)(2,1)S(1)} %copy.112) | copy-start | bytes 2359300
  366.2 73.1 %copy-start.9 = (bf16[128,4,1,768]{0,3,1,2:T(8,128)(2,1)}, bf16[128,4,1,768]{0,3,1,2:T(8,128)(2,1)S(1)}, u32[]{:S(2)}) copy-start(bf16[128,4,1,768]{0,3,1,2:T(8,128)(2,1)S(1)} %copy.106) | copy-start | bytes 2359300
  429.4 126.7 %copy-start.1 = (bf16[128,2048]{1,0:T(8,128)(2,1)S(1)}, bf16[128,2048]{1,0:T(8,128)(2,1)}, u32[]{:S(2)}) copy-start(bf16[128,2048]{1,0:T(8,128)(2,1)} %copy-done) | copy-start | bytes 1572868
  429.4 126.7 %copy-start.17 = (f32[2048]{0:T(1024)S(1)}, f32[2048]{0:T(1024)}, u32[]{:S(2)}) copy-start(f32[2048]{0:T(1024)} %param.22) | copy-start | bytes 24580
  429.4 126.7 %copy-start.18 = (f32[2048]{0:T(1024)S(1)}, f32[2048]{0:T(1024)}, u32[]{:S(2)}) copy-start(f32[2048]{0:T(1024)} %param.23) | copy-start | bytes 24580
  429.4 126.7 %copy-start.21 = (f32[4096]{0:T(1024)S(1)}, f32[4096]{0:T(1024)}, u32[]{:S(2)}) copy-start(f32[4096]{0:T(1024)} %param.29) | copy-start | bytes 49156
  439.3 243.4 %copy-start.8 = (bf16[128,2048]{1,0:T(8,128)(2,1)S(1)}, bf16[128,2048]{1,0:T(8,128)(2,1)}, u32[]{:S(2)}) copy-start(bf16[128,2048]{1,0:T(8,128)(2,1)} %copy-done.7) | copy-start | bytes 1572868
  706.3 169.0 %reduce-scatter.13.cloned.1.call-start = ((), (), s32[]{:S(2)}) async-start(), calls=%async_computation.18 | async-start | bytes 8912896 | tf_op jit(solution)/shard_map/reduce_scatter | solution.py:296
  730.3 167.9 %reduce-scatter.7.cloned.1.call-start = ((), (), s32[]{:S(2)}) async-start(), calls=%async_computation.14 | async-start | bytes 1572864 | tf_op jit(solution)/shard_map/reduce_scatter | solution.py:198
  748.2 243.4 %all-reduce.5.cloned.1.call-start = ((), (), s32[]{:S(2)}) async-start(), calls=%async_computation.21 | async-start | bytes 131072 | tf_op jit(solution)/shard_map/psum | solution.py:308
  767.6 3.0 copy-start.15
  772.2 555.9 %reduce-scatter.17.cloned.1.call-start = ((), (), s32[]{:S(2)}) async-start(), calls=%async_computation.20 | async-start | bytes 35651584 | tf_op jit(solution)/shard_map/reduce_scatter | solution.py:298
  788.3 1.2 copy-start.10
  788.3 787.0 %reduce-scatter.11.cloned.1.call-start = ((), (), s32[]{:S(2)}) async-start(), calls=%async_computation.17 | async-start | bytes 26738688 | tf_op jit(solution)/shard_map/reduce_scatter | solution.py:295
  800.1 1.2 copy-start.12
  800.1 1109.7 %reduce-scatter.15.cloned.1.call-start = ((), (), s32[]{:S(2)}) async-start(), calls=%async_computation.19 | async-start | bytes 35651584 | tf_op jit(solution)/shard_map/reduce_scatter | solution.py:297
  814.6 83.6 %copy-start.16 = (bf16[128,1024]{1,0:T(8,128)(2,1)S(1)}, bf16[128,1024]{1,0:T(8,128)(2,1)}, u32[]{:S(2)}) copy-start(bf16[128,1024]{1,0:T(8,128)(2,1)} %param.18) | copy-start | bytes 786436
  814.6 83.6 %copy-start.30 = (f32[1024]{0:T(1024)S(1)}, f32[1024]{0:T(1024)}, u32[]{:S(2)}) copy-start(f32[1024]{0:T(1024)} %param.31) | copy-start | bytes 12292
  814.6 83.6 %copy-start.31 = (f32[1024]{0:T(1024)S(1)}, f32[1024]{0:T(1024)}, u32[]{:S(2)}) copy-start(f32[1024]{0:T(1024)} %param.27) | copy-start | bytes 12292
  991.6 918.1 %copy-start.23 = (f32[1024]{0:T(1024)S(1)}, f32[1024]{0:T(1024)}, u32[]{:S(2)}) copy-start(f32[1024]{0:T(1024)} %get-tuple-element.611) | copy-start | bytes 12292
  991.6 918.7 %copy-start.29 = (f32[2048]{0:T(1024)S(1)}, f32[2048]{0:T(1024)}, u32[]{:S(2)}) copy-start(f32[2048]{0:T(1024)} %get-tuple-element.604) | copy-start | bytes 24580
  991.6 919.3 %copy-start.28 = (f32[2048]{0:T(1024)S(1)}, f32[2048]{0:T(1024)}, u32[]{:S(2)}) copy-start(f32[2048]{0:T(1024)} %get-tuple-element.605) | copy-start | bytes 24580
  991.7 919.9 %copy-start.27 = (f32[2048]{0:T(1024)S(1)}, f32[2048]{0:T(1024)}, u32[]{:S(2)}) copy-start(f32[2048]{0:T(1024)} %get-tuple-element.606) | copy-start | bytes 24580
  991.7 920.5 %copy-start.26 = (f32[2048]{0:T(1024)S(1)}, f32[2048]{0:T(1024)}, u32[]{:S(2)}) copy-start(f32[2048]{0:T(1024)} %get-tuple-element.607) | copy-start | bytes 24580
  991.7 921.1 %copy-start.25 = (f32[3072]{0:T(1024)S(1)}, f32[3072]{0:T(1024)}, u32[]{:S(2)}) copy-start(f32[3072]{0:T(1024)} %get-tuple-element.609) | copy-start | bytes 36868
  991.7 922.3 %copy-start.22 = (f32[4096]{0:T(1024)S(1)}, f32[4096]{0:T(1024)}, u32[]{:S(2)}) copy-start(f32[4096]{0:T(1024)} %get-tuple-element.613) | copy-start | bytes 49156
  (1 other events, 0.8 us)
Sparse Core Ops, SparseCore 0:
  28.2 71.4 all-gather.7
  193.6 27.8 all-gather.5
  267.4 44.4 reduce-scatter.8
  314.0 115.3 all-gather.13
  431.4 124.6 all-gather.9
  558.1 124.5 all-gather.11
  706.4 61.1 all-reduce.6
  771.7 103.5 reduce-scatter.12
  878.1 20.0 reduce-scatter.6
  903.7 87.9 all-reduce.4
  995.9 332.0 reduce-scatter.16
  1332.6 242.6 reduce-scatter.10
  1580.1 329.6 reduce-scatter.14
